TPU v7x, 32 devices: a whole 2x2x4 slice. The times are simulated.
32 devices in a mesh: pages: 8 (over y, x, core), heads: 4 (over z).
Axes of the slice: x: 2, y: 2, z: 4, core: 2. Of those that a mesh axis runs over, the one named last changes fastest.
Arguments:
- queries: bfloat16 [512, 32, 128], P('pages', 'heads'), may hold values from -6 to 6
- keys: bfloat16 [576, 16, 128, 128], P('pages', 'heads'), may hold values from -6 to 6
- values: bfloat16 [576, 16, 128, 128], P('pages', 'heads'), may hold values from -6 to 6
- hot_pages: int32 [64], replicated, may hold values from 0 to 575, as said below
- hot_used: int32 [512], replicated, may hold values from 1 to 64
- user_pages: int32 [512, 1], P('pages'), may hold values from 8 to 71, as said below
- lengths: int32 [512], P('pages'), may hold values from 1 to 128
- o_weight: bfloat16 [4096, 4608], P('heads'), may hold values from -0.09375 to 0.09375
- residual: bfloat16 [512, 4608], P(('pages', 'heads')), may hold values from -6 to 6
- norm_gain: float32 [4608], replicated, may hold values from 0.25 to 1.75
Outputs:
- output: bfloat16 [512, 4608], P(('pages', 'heads'))
Inputs may be any that keep to these rules, and one draw needn't show every extreme that they name: `hot_pages`: 64 distinct pages; each lies among the first 8 pages of its group (page p belongs to group p // 72); one group holds exactly 8 of them and none holds more. `user_pages`: numbers within the sequence's own group (sequence s belongs to group s // 64); all own pages of the sequences of one group are distinct.
All inputs are finite; a program needn't handle non-finite values.
Results may differ from a plain program's by a relative error of at most 0.019.
Values may be sent and summed in bfloat16 or wider, within the bound.
No kernel may reach another device: no remote copies, remote signals or barrier semaphores. Data moves between devices by JAX's collectives and lax.ppermute only.
A program may use at most 128 MiB of HBM per device.

v0:
```python
import jax
import jax.numpy as jnp
from jax import lax
from jax.sharding import PartitionSpec as P

HOT_CAP = 8
score_scale = 1.0 / 12.0
soft_cap = 50.0
epsilon = 1e-06


def shared_terms(grouped, page_keys, page_values, allowed):
    logits = jnp.einsum("skgd,pktd->skgpt", grouped, page_keys, preferred_element_type=jnp.float32)
    weight = jnp.exp(soft_cap * jnp.tanh(logits * (score_scale / soft_cap)))
    weight = jnp.where(allowed[:, None, None, :, None], weight, 0.0)
    numerator = jnp.einsum(
        "skgpt,pktd->skgd",
        weight.astype(jnp.bfloat16),
        page_values,
        preferred_element_type=jnp.float32,
    )
    return (numerator, jnp.sum(weight, axis=(3, 4)))


def own_terms(grouped, owned_keys, owned_values, lengths):
    logits = jnp.einsum(
        "skgd,suktd->skgut", grouped, owned_keys, preferred_element_type=jnp.float32
    )
    page_len = owned_keys.shape[3]
    token_pos = (
        jnp.arange(owned_keys.shape[1], dtype=jnp.int32)[:, None] * page_len
        + jnp.arange(page_len, dtype=jnp.int32)[None, :]
    )
    allowed = token_pos[None, :, :] < lengths[:, None, None]
    weight = jnp.exp(soft_cap * jnp.tanh(logits * (score_scale / soft_cap)))
    weight = jnp.where(allowed[:, None, None, :, :], weight, 0.0)
    numerator = jnp.einsum(
        "skgut,suktd->skgd",
        weight.astype(jnp.bfloat16),
        owned_values,
        preferred_element_type=jnp.float32,
    )
    return (numerator, jnp.sum(weight, axis=(3, 4)))


def slot_places(page_ids, hot_pages):
    hot_order = jnp.arange(hot_pages.shape[0], dtype=jnp.int32)
    matches = page_ids[:, None] == hot_pages[None, :]
    present = jnp.any(matches, axis=1)
    position = jnp.sum(jnp.where(matches, hot_order[None, :], 0), axis=1)
    return (present, position)


def per_device(
    queries, keys, values, hot_pages, hot_used, user_pages, lengths, o_weight, residual, norm_gain
):
    seq_dev, head_count, head_dim = queries.shape
    kv_heads = keys.shape[1]
    group_size = head_count // kv_heads
    page_count = keys.shape[0]
    grouped = queries.reshape(seq_dev, kv_heads, group_size, head_dim)
    myself = lax.axis_index("pages")
    hot_keys = keys[:HOT_CAP]
    hot_values = values[:HOT_CAP]
    everyone = lax.all_gather(queries, "pages", axis=0, tiled=True)
    page_ids = myself * page_count + jnp.arange(HOT_CAP, dtype=jnp.int32)
    present, position = slot_places(page_ids, hot_pages)
    allowed = present[None, :] & (position[None, :] < hot_used[:, None])
    everyone_grouped = everyone.reshape(everyone.shape[0], kv_heads, group_size, head_dim)
    numerator, totals = shared_terms(everyone_grouped, hot_keys, hot_values, allowed)
    numerator, totals = (
        lax.psum_scatter(
            numerator.astype(jnp.bfloat16), "pages", scatter_dimension=0, tiled=True
        ).astype(jnp.float32),
        lax.psum_scatter(
            totals.astype(jnp.bfloat16), "pages", scatter_dimension=0, tiled=True
        ).astype(jnp.float32),
    )
    owned_keys = keys[user_pages]
    owned_values = values[user_pages]
    own_numerator, own_totals = own_terms(grouped, owned_keys, owned_values, lengths)
    attended = ((numerator + own_numerator) / (totals + own_totals)[:, :, :, None]).astype(
        jnp.bfloat16
    )
    attended = attended.reshape(seq_dev, head_count * head_dim)
    projected = lax.psum_scatter(
        jnp.dot(attended, o_weight, preferred_element_type=jnp.float32).astype(jnp.bfloat16),
        "heads",
        scatter_dimension=0,
        tiled=True,
    ).astype(jnp.float32)
    mean_sq = jnp.mean(projected * projected, axis=1, keepdims=True)
    normed = projected / jnp.sqrt(mean_sq + epsilon) * norm_gain[None, :]
    return (residual.astype(jnp.float32) + normed).astype(jnp.bfloat16)


def solution(mesh):
    in_specs = (
        P("pages", "heads", None),
        P("pages", "heads", None, None),
        P("pages", "heads", None, None),
        P(),
        P(),
        P("pages", None),
        P("pages"),
        P("heads", None),
        P(("pages", "heads"), None),
        P(),
    )
    out_specs = P(("pages", "heads"), None)
    return jax.shard_map(
        per_device, mesh=mesh, in_specs=in_specs, out_specs=out_specs, check_vma=False
    )
```

profile of v0, /device:TPU:0, one launch (start us, length us, event | category | flops | bytes accessed | tf_op | source)
XLA Modules:
  0.0 159.2 jit_solution(6237646934203751264)
XLA Ops:
  6.5 0.7 all-gather.2.cloned.1.call-update
  7.3 0.0 reduce-scatter.10.cloned.1.call-start
  7.3 0.7 fusion.27
  8.0 9.2 %gather_fusion = bf16[64,4,128,128]{3,2,1,0:T(8,128)(2,1)} fusion(bf16[72,4,128,128]{3,2,1,0:T(8,128)(2,1)} %param.11, s32[1024]{0:T(1024)S(1)} %pad_clamp_fusion), kind=kCustom, calls=%fused_computation | custom fusion | bytes 16777472 | tf_op jit(solution)/shard_map/gather | solution.py:79
  17.2 9.4 %gather_fusion.1 = bf16[64,4,128,128]{3,2,1,0:T(8,128)(2,1)} fusion(bf16[72,4,128,128]{3,2,1,0:T(8,128)(2,1)} %param.12, s32[1024]{0:T(1024)S(1)} %pad_clamp_fusion), kind=kCustom, calls=%fused_computation.1 | custom fusion | bytes 16777472 | tf_op jit(solution)/shard_map/gather | solution.py:80
  26.6 0.2 compare_reduce_fusion
  26.8 0.2 fusion.26
  26.9 0.1 compare_and_fusion
  27.0 8.3 %all-gather.2.cloned.1.call-done = bf16[512,8,128]{2,1,0:T(8,128)(2,1)} async-done(((bf16[64,8,128]{2,1,0:T(8,128)(2,1)}), bf16[512,8,128]{2,1,0:T(8,128)(2,1)}) %all-gather.2.cloned.1.call-update) | async-done | bytes 1048592 | tf_op jit(solution)/shard_map/all_gather | solution.py:65
  35.3 1.4 copy.39
  36.7 9.5 %fusion = (bf16[512,4,2]{0,2,1:T(2,128)(2,1)S(1)}, f32[4,8,128,512,2]{3,2,4,1,0:T(8,128)}) fusion(pred[512,8]{0,1:T(8,128)(4,1)S(1)} %compare_and_fusion, bf16[512,4,2,128,1]{3,0,2,4,1:T(8,128)(2,1)S(1)} %bitcast.55, bf16[72,4,128,128]{3,2,1,0:T(8,128)(2,1)} %param.11), kind=kOutput, calls=%fused_computation.3 | convolution fusion | flops 1090514944 | bytes 18886656 | tf_op jit(solution)/shard_map/skgd,pktd->skgpt/dot_general | solution.py:13
  46.2 0.8 copy.55
  47.0 0.0 reduce-scatter.10.cloned.1.call-update
  47.0 0.0 reduce-scatter.6.cloned.1.call-start
  47.1 10.1 %fusion.7 = bf16[512,4,2,128]{3,0,2,1:T(8,128)(2,1)} fusion(f32[4,8,128,512,2]{3,2,4,1,0:T(8,128)} %get-tuple-element.8, pred[512,8]{0,1:T(8,128)(4,1)S(1)} %compare_and_fusion, bf16[72,4,128,128]{3,2,1,0:T(8,128)(2,1)} %param.12), kind=kOutput, calls=%fused_computation.9 | convolution fusion | flops 1091043328 | bytes 18878464 | tf_op jit(solution)/shard_map/skgpt,pktd->skgd/dot_general | solution.py:16
  57.2 0.0 reduce-scatter.6.cloned.1.call-update
  57.2 0.2 reduce-scatter.8.cloned.1.call-start
  57.5 0.1 iota_compare_fusion
  57.5 8.0 %fusion.31 = (f32[64,4,2]{2,1,0:T(4,128)S(1)}, bf16[64,4,2,128]{3,2,1,0:T(2,128)(2,1)S(1)}) fusion(bf16[64,4,128,128]{3,2,1,0:T(8,128)(2,1)} %gather_fusion, bf16[64,4,2,128]{3,2,1,0:T(2,128)(2,1)S(1)} %bitcast.56, pred[64,128]{1,0:T(8,128)(4,1)S(1)} %iota_compare_fusion), kind=kOutput, calls=%fused_computation.45 | convolution fusion | flops 17104384 | bytes 8660992 | tf_op jit(solution)/shard_map/skgd,suktd->skgut/dot_general | solution.py:26
  65.5 0.1 copy.44
  65.6 5.7 %fusion.24 = f32[64,4,2,128]{3,2,1,0:T(2,128)S(1)} fusion(bf16[64,4,128,128]{3,2,1,0:T(8,128)(2,1)} %gather_fusion.1, bf16[64,4,2,128]{3,2,1,0:T(2,128)(2,1)S(1)} %get-tuple-element.6), kind=kOutput, calls=%fused_computation.29 | convolution fusion | flops 16777216 | bytes 8781824 | tf_op jit(solution)/shard_map/skgut,suktd->skgd/dot_general | solution.py:37
  71.3 9.6 %reduce-scatter.10.cloned.1.call-done = bf16[64,8]{1,0:T(8,128)(2,1)} async-done(((bf16[512,8]{1,0:T(8,128)(2,1)}), bf16[64,8]{1,0:T(8,128)(2,1)}) %reduce-scatter.10.cloned.1.call-update) | async-done | bytes 1040
  80.9 0.8 copy.56
  81.7 38.4 %reduce-scatter.6.cloned.1.call-done = bf16[64,4,2,128]{3,0,2,1:T(8,128)(2,1)} async-done(((bf16[512,4,2,128]{3,0,2,1:T(8,128)(2,1)}), bf16[64,4,2,128]{3,0,2,1:T(8,128)(2,1)}) %reduce-scatter.6.cloned.1.call-update) | async-done | bytes 131088 | tf_op jit(solution)/shard_map/reduce_scatter | solution.py:72
  120.1 1.0 fusion.23
  121.1 0.1 copy.46
  121.3 0.1 reshape.104
  121.3 6.2 %convolution_convert_fusion = bf16[64,4608]{1,0:T(8,128)(2,1)} fusion(bf16[64,1024]{1,0:T(8,128)(2,1)S(1)} %reshape.104, bf16[1024,4608]{1,0:T(8,128)(2,1)} %param.17), kind=kOutput, calls=%fused_computation.7 | convolution fusion | flops 604274688 | bytes 10158080 | tf_op jit(solution)/shard_map/dot_general | solution.py:87
  127.6 0.0 reduce-scatter.8.cloned.1.call-update
  127.6 22.3 %reduce-scatter.8.cloned.1.call-done = bf16[16,4608]{1,0:T(8,128)(2,1)} async-done(((bf16[64,4608]{1,0:T(8,128)(2,1)}), bf16[16,4608]{1,0:T(8,128)(2,1)}) %reduce-scatter.8.cloned.1.call-update) | async-done | bytes 147472 | tf_op jit(solution)/shard_map/reduce_scatter | solution.py:86
  149.9 1.1 fusion.18
  151.0 1.7 %fusion.21 = bf16[16,4608]{1,0:T(8,128)(2,1)} fusion(bf16[16,4608]{1,0:T(8,128)(2,1)} %reduce-scatter.8.cloned.1.call-done, bf16[16,4608]{1,0:T(8,128)(2,1)S(1)} %copy-done, f32[4608]{0:T(1024)S(1)} %copy-done.2, f32[16]{0:T(128)S(1)} %add_sqrt_fusion), kind=kLoop, calls=%fused_computation.25 | loop fusion | flops 442368 | bytes 460864 | tf_op jit(solution)/shard_map/convert_element_type | solution.py:94
  (19 shorter events, 0.1 us)
Async XLA Ops:
  6.5 28.8 %all-gather.2.cloned.1.call-start = ((), (), s32[]{:S(2)}) async-start(), calls=%async_computation.3 | async-start | bytes 1179648 | tf_op jit(solution)/shard_map/all_gather | solution.py:65
  7.3 73.7 %reduce-scatter.10.cloned.1.call-start = ((), (), s32[]{:S(2)}) async-start(), calls=%async_computation.6 | async-start | bytes 147456
  17.2 9.4 %copy-start.5 = (s32[64]{0:T(128)S(1)}, s32[64]{0:T(128)}, u32[]{:S(2)}) copy-start(s32[64]{0:T(128)} %param.13) | copy-start | bytes 772
  17.2 9.8 %copy-start.3 = (s32[512]{0:T(512)S(1)}, s32[512]{0:T(512)}, u32[]{:S(2)}) copy-start(s32[512]{0:T(512)} %param.14) | copy-start | bytes 6148
  47.0 73.0 %reduce-scatter.6.cloned.1.call-start = ((), (), s32[]{:S(2)}) async-start(), calls=%async_computation.4 | async-start | bytes 1179648 | tf_op jit(solution)/shard_map/reduce_scatter | solution.py:72
  47.1 10.4 %copy-start.4 = (s32[64]{0:T(128)S(1)}, s32[64]{0:T(128)}, u32[]{:S(2)}) copy-start(s32[64]{0:T(128)} %param.16) | copy-start | bytes 772
  47.1 10.4 %copy-start.1 = (bf16[64,8,128]{2,1,0:T(8,128)(2,1)S(1)}, bf16[64,8,128]{2,1,0:T(8,128)(2,1)}, u32[]{:S(2)}) copy-start(bf16[64,8,128]{2,1,0:T(8,128)(2,1)} %param.10) | copy-start | bytes 393220
  57.2 92.7 %reduce-scatter.8.cloned.1.call-start = ((), (), s32[]{:S(2)}) async-start(), calls=%async_computation.5 | async-start | bytes 737280 | tf_op jit(solution)/shard_map/reduce_scatter | solution.py:86
  71.3 79.7 %copy-start = (bf16[16,4608]{1,0:T(8,128)(2,1)S(1)}, bf16[16,4608]{1,0:T(8,128)(2,1)}, u32[]{:S(2)}) copy-start(bf16[16,4608]{1,0:T(8,128)(2,1)} %param.18) | copy-start | bytes 442372
  71.3 79.7 %copy-start.2 = (f32[4608]{0:T(1024)S(1)}, f32[4608]{0:T(1024)}, u32[]{:S(2)}) copy-start(f32[4608]{0:T(1024)} %param.19) | copy-start | bytes 55300
Sparse Core Ops, SparseCore 0:
  9.2 26.0 all-gather.1
  47.2 33.6 reduce-scatter.9
  84.1 35.9 reduce-scatter.5
  127.7 22.1 reduce-scatter.7
where the time goes:
time: 160 us; the launch traced here: 159 us
  waiting for transfers between devices  79.3 us (50%)
  matrix products  39.5 us (25%)
  local copies, waits for them, and re-layouts  21.9 us (14%)
  between operations  13.2 us (8%)
  other arithmetic  5 us (3%)
    reduce_scatter x1, waiting for transfers between devices, per_device(): lax.psum_scatter(numerator.astype(jnp.bfloat16), 'pages', scatter_dimensi...  38.4 us
    reduce_scatter x1, waiting for transfers between devices, per_device(): lax.psum_scatter(jnp.dot(attended, o_weight, preferred_element_type=jnp.f...  22.3 us
    unnamed x5, waiting for transfers between devices  10.3 us
    dot_general x1, matrix products, shared_terms(): jnp.einsum('skgpt,pktd->skgd', weight.astype(jnp.bfloat16), page_values,...  10.1 us
    dot_general x1, matrix products, shared_terms(): jnp.einsum('skgd,pktd->skgpt', grouped, page_keys, preferred_element_type...  9.5 us
    gather x1, local copies, waits for them, and re-layouts, per_device(): owned_values = values[user_pages]  9.39 us
    gather x1, local copies, waits for them, and re-layouts, per_device(): owned_keys = keys[user_pages]  9.2 us
    all_gather x1, waiting for transfers between devices, per_device(): everyone = lax.all_gather(queries, 'pages', axis=0, tiled=True)  8.32 us
  transfers between devices with their start and end apart: 4, of which 4 were waited for; matrix products, arithmetic and copies ran while one was open for 28% of the time, Pallas kernels for 0%

commit v1 on v0

--- a/solution.py
+++ b/solution.py
@@ -62,7 +62,24 @@
     myself = lax.axis_index("pages")
     hot_keys = keys[:HOT_CAP]
     hot_values = values[:HOT_CAP]
-    everyone = lax.all_gather(queries, "pages", axis=0, tiled=True)
+    size, index, rows = (lax.axis_size("pages"), lax.axis_index("pages"), queries.shape[0])
+    forward = [(i, (i + 1) % size) for i in range(size)]
+    behind = [(i, (i - 1) % size) for i in range(size)]
+    filled = jnp.zeros((*queries.shape[:0], size * rows, *queries.shape[0 + 1 :]), queries.dtype)
+    filled = lax.dynamic_update_slice_in_dim(filled, queries, index * rows, axis=0)
+    from_left = from_right = queries
+    halfway = size // 2
+    for hop in range(1, halfway + 1):
+        from_left = lax.ppermute(from_left, "pages", forward)
+        filled = lax.dynamic_update_slice_in_dim(
+            filled, from_left, (index - hop) % size * rows, axis=0
+        )
+        if hop < size - halfway:
+            from_right = lax.ppermute(from_right, "pages", behind)
+            filled = lax.dynamic_update_slice_in_dim(
+                filled, from_right, (index + hop) % size * rows, axis=0
+            )
+    everyone = filled
     page_ids = myself * page_count + jnp.arange(HOT_CAP, dtype=jnp.int32)
     present, position = slot_places(page_ids, hot_pages)
     allowed = present[None, :] & (position[None, :] < hot_used[:, None])

time: 160 us -> 173 us (1.081)
  starting transfers between devices: 0.31 us -> 8.92 us
  waiting for transfers between devices: 79.3 us -> 83.4 us
    ppermute x0 -> x7, waiting for transfers between devices: none -> 10.6 us  [the longest x4 10.6 us: per_device(): from_left = lax.ppermute(from_left, 'pages', forward)]
    ppermute x0 -> x7, starting transfers between devices: none -> 8.65 us  [the longest x3 8.14 us: per_device(): from_right = lax.ppermute(from_right, 'pages', behind)]
    all_gather x1 -> x0, waiting for transfers between devices: 8.32 us -> none  [per_device(): everyone = lax.all_gather(queries, 'pages', axis=0, tiled=True)]
    unnamed x5 -> x4, waiting for transfers between devices: 10.3 us -> 12.1 us
  transfers between devices with their start and end apart: 4 -> 10, of which waited for: 4 -> 6; matrix products, arithmetic and copies ran while one was open for 28% -> 27% of each run, Pallas kernels for 0% -> 0%
where the time goes in v1:
time: 173 us; the launch traced here: 172 us
  waiting for transfers between devices  83.4 us (48%)
  matrix products  39.5 us (23%)
  local copies, waits for them, and re-layouts  20.8 us (12%)
  between operations  13.3 us (8%)
  starting transfers between devices  8.92 us (5%)
  other arithmetic  6.31 us (4%)
    reduce_scatter x1, waiting for transfers between devices, per_device(): lax.psum_scatter(numerator.astype(jnp.bfloat16), 'pages', scatter_dimensi...  38.4 us
    reduce_scatter x1, waiting for transfers between devices, per_device(): lax.psum_scatter(jnp.dot(attended, o_weight, preferred_element_type=jnp.f...  22.3 us
    unnamed x4, waiting for transfers between devices  12.1 us
    ppermute x4, waiting for transfers between devices, per_device(): from_left = lax.ppermute(from_left, 'pages', forward)  10.6 us
    dot_general x1, matrix products, shared_terms(): jnp.einsum('skgpt,pktd->skgd', weight.astype(jnp.bfloat16), page_values,...  10.1 us
    dot_general x1, matrix products, shared_terms(): jnp.einsum('skgd,pktd->skgpt', grouped, page_keys, preferred_element_type...  9.51 us
    gather x1, local copies, waits for them, and re-layouts, per_device(): owned_keys = keys[user_pages]  9.23 us
    gather x1, local copies, waits for them, and re-layouts, per_device(): owned_values = values[user_pages]  9.21 us
  transfers between devices with their start and end apart: 10, of which 6 were waited for; matrix products, arithmetic and copies ran while one was open for 27% of the time, Pallas kernels for 0%

profile of v1, /device:TPU:0, one launch (start us, length us, event | category | flops | bytes accessed | tf_op | source)
XLA Modules:
  0.0 172.2 jit_solution(1971294753507689)
XLA Ops:
  6.5 0.5 collective-permute-start
  7.0 2.9 %collective-permute-start.1 = (bf16[64,8,128]{2,1,0:T(8,128)(2,1)}, bf16[64,8,128]{2,1,0:T(8,128)(2,1)S(1)}, u32[]{:S(2)}, u32[]{:S(2)}) collective-permute-start(bf16[64,8,128]{2,1,0:T(8,128)(2,1)} %param.10), channel_id=1, source_target_pairs={{0,28},{4,0},{8,4},{12,8},{16,12},{20,16},{24,20},{28,24},{1,29},{... | collective-permute-start | bytes 393224 | tf_op jit(solution)/shard_map/ppermute | solution.py:78
  9.9 0.8 fusion.17
  10.7 0.8 compare_reduce_fusion
  11.6 0.7 fusion.18
  12.3 9.2 %gather_fusion.1 = bf16[64,4,128,128]{3,2,1,0:T(8,128)(2,1)} fusion(bf16[72,4,128,128]{3,2,1,0:T(8,128)(2,1)} %param.12, s32[1024]{0:T(1024)S(1)} %pad_clamp_fusion), kind=kCustom, calls=%fused_computation.1 | custom fusion | bytes 16777472 | tf_op jit(solution)/shard_map/gather | solution.py:97
  21.5 9.2 %gather_fusion = bf16[64,4,128,128]{3,2,1,0:T(8,128)(2,1)} fusion(bf16[72,4,128,128]{3,2,1,0:T(8,128)(2,1)} %param.11, s32[1024]{0:T(1024)S(1)} %pad_clamp_fusion), kind=kCustom, calls=%fused_computation | custom fusion | bytes 16777472 | tf_op jit(solution)/shard_map/gather | solution.py:96
  30.7 0.1 broadcast_in_dim.58
  30.9 0.1 compare_and_fusion
  31.0 2.6 %collective-permute-start.3 = (bf16[64,8,128]{2,1,0:T(8,128)(2,1)S(1)}, bf16[64,8,128]{2,1,0:T(8,128)(2,1)S(1)}, u32[]{:S(2)}, u32[]{:S(2)}) collective-permute-start(bf16[64,8,128]{2,1,0:T(8,128)(2,1)S(1)} %collective-permute-done.1), channel_id=1, source_target_pairs={{0,28},{4,0},{8,4},{12,8},{16,12},{20,16},{24,20},{28,24},{1,29},{... | collective-permute-start | bytes 393224 | tf_op jit(solution)/shard_map/ppermute | solution.py:78
  33.7 2.6 %collective-permute-done.2 = bf16[64,8,128]{2,1,0:T(8,128)(2,1)S(1)} collective-permute-done((bf16[64,8,128]{2,1,0:T(8,128)(2,1)S(1)}, bf16[64,8,128]{2,1,0:T(8,128)(2,1)S(1)}, u32[]{:S(2)}, u32[]{:S(2)}) %collective-permute-start.2) | collective-permute-done | bytes 131104 | tf_op jit(solution)/shard_map/ppermute | solution.py:73
  36.3 2.6 %collective-permute-start.5 = (bf16[64,8,128]{2,1,0:T(8,128)(2,1)S(1)}, bf16[64,8,128]{2,1,0:T(8,128)(2,1)S(1)}, u32[]{:S(2)}, u32[]{:S(2)}) collective-permute-start(bf16[64,8,128]{2,1,0:T(8,128)(2,1)S(1)} %collective-permute-done.3), channel_id=1, source_target_pairs={{0,28},{4,0},{8,4},{12,8},{16,12},{20,16},{24,20},{28,24},{1,29},{... | collective-permute-start | bytes 393224 | tf_op jit(solution)/shard_map/ppermute | solution.py:78
  39.0 2.9 %collective-permute-done.4 = bf16[64,8,128]{2,1,0:T(8,128)(2,1)S(1)} collective-permute-done((bf16[64,8,128]{2,1,0:T(8,128)(2,1)S(1)}, bf16[64,8,128]{2,1,0:T(8,128)(2,1)S(1)}, u32[]{:S(2)}, u32[]{:S(2)}) %collective-permute-start.4) | collective-permute-done | bytes 131104 | tf_op jit(solution)/shard_map/ppermute | solution.py:73
  42.0 5.2 %collective-permute-done.6 = bf16[64,8,128]{2,1,0:T(8,128)(2,1)S(1)} collective-permute-done((bf16[64,8,128]{2,1,0:T(8,128)(2,1)S(1)}, bf16[64,8,128]{2,1,0:T(8,128)(2,1)S(1)}, u32[]{:S(2)}, u32[]{:S(2)}) %collective-permute-start.6) | collective-permute-done | bytes 131104 | tf_op jit(solution)/shard_map/ppermute | solution.py:73
  47.2 9.5 %bitcast_reduce_fusion = (bf16[512,4,2]{0,2,1:T(2,128)(2,1)S(1)}, f32[4,512,2,8,128]{1,4,3,2,0:T(8,128)}) fusion(pred[512,8]{0,1:T(8,128)(4,1)S(1)} %compare_and_fusion, bf16[512,4,2,128,1]{3,0,4,2,1:T(8,128)(2,1)S(1)} %bitcast.48, bf16[72,4,128,128]{3,2,1,0:T(8,128)(2,1)} %param.11), kind=kOutput, calls=%fused_computation.2 | convolution fusion | flops 1090514944 | bytes 18886656 | tf_op jit(solution)/shard_map/skgd,pktd->skgpt/dot_general | solution.py:13
  56.7 0.8 copy.89
  57.6 10.1 %fusion.2 = bf16[512,4,2,128]{3,0,2,1:T(8,128)(2,1)} fusion(f32[4,512,2,8,128]{1,4,3,2,0:T(8,128)} %get-tuple-element.8, pred[512,8]{0,1:T(8,128)(4,1)S(1)} %compare_and_fusion, bf16[72,4,128,128]{3,2,1,0:T(8,128)(2,1)} %param.12), kind=kOutput, calls=%fused_computation.9 | convolution fusion | flops 1091043328 | bytes 18878464 | tf_op jit(solution)/shard_map/skgpt,pktd->skgd/dot_general | solution.py:16
  67.7 0.2 reduce-scatter.8.cloned.1.call-start
  68.0 0.1 iota_compare_fusion
  68.0 8.0 %fusion.22 = (f32[64,4,2]{2,1,0:T(4,128)S(1)}, bf16[64,4,2,128]{3,2,1,0:T(2,128)(2,1)S(1)}) fusion(bf16[64,4,128,128]{3,2,1,0:T(8,128)(2,1)} %gather_fusion, bf16[64,4,2,128]{3,2,1,0:T(2,128)(2,1)S(1)} %bitcast.49, pred[64,128]{1,0:T(8,128)(4,1)S(1)} %iota_compare_fusion), kind=kOutput, calls=%fused_computation.52 | convolution fusion | flops 17104384 | bytes 8660992 | tf_op jit(solution)/shard_map/skgd,suktd->skgut/dot_general | solution.py:26
  76.1 0.1 copy.79
  76.2 5.7 %fusion.15 = f32[64,4,2,128]{3,2,1,0:T(2,128)S(1)} fusion(bf16[64,4,128,128]{3,2,1,0:T(8,128)(2,1)} %gather_fusion.1, bf16[64,4,2,128]{3,2,1,0:T(2,128)(2,1)S(1)} %get-tuple-element.6), kind=kOutput, calls=%fused_computation.36 | convolution fusion | flops 16777216 | bytes 8781824 | tf_op jit(solution)/shard_map/skgut,suktd->skgd/dot_general | solution.py:37
  81.8 12.0 %reduce-scatter.10.cloned.1.call-done = bf16[64,8]{1,0:T(8,128)(2,1)} async-done(((bf16[512,8]{1,0:T(8,128)(2,1)}), bf16[64,8]{1,0:T(8,128)(2,1)}) %reduce-scatter.10.cloned.1.call-update) | async-done | bytes 1040
  93.9 0.8 copy.90
  94.7 38.4 %reduce-scatter.6.cloned.1.call-done = bf16[64,4,2,128]{3,0,2,1:T(8,128)(2,1)} async-done(((bf16[512,4,2,128]{3,0,2,1:T(8,128)(2,1)}), bf16[64,4,2,128]{3,0,2,1:T(8,128)(2,1)}) %reduce-scatter.6.cloned.1.call-update) | async-done | bytes 131088 | tf_op jit(solution)/shard_map/reduce_scatter | solution.py:89
  133.0 1.0 fusion.14
  134.1 0.1 copy.81
  134.2 0.1 reshape.104
  134.3 6.2 %convolution_convert_fusion = bf16[64,4608]{1,0:T(8,128)(2,1)} fusion(bf16[64,1024]{1,0:T(8,128)(2,1)S(1)} %reshape.104, bf16[1024,4608]{1,0:T(8,128)(2,1)} %param.17), kind=kOutput, calls=%fused_computation.7 | convolution fusion | flops 604274688 | bytes 10158080 | tf_op jit(solution)/shard_map/dot_general | solution.py:104
  140.6 22.3 %reduce-scatter.8.cloned.1.call-done = bf16[16,4608]{1,0:T(8,128)(2,1)} async-done(((bf16[64,4608]{1,0:T(8,128)(2,1)}), bf16[16,4608]{1,0:T(8,128)(2,1)}) %reduce-scatter.8.cloned.1.call-update) | async-done | bytes 147472 | tf_op jit(solution)/shard_map/reduce_scatter | solution.py:103
  162.8 1.1 fusion.9
  163.9 1.7 fusion.12
  (36 shorter events, 0.5 us)
Async XLA Ops:
  6.5 87.3 %reduce-scatter.10.cloned.1.call-start = ((), (), s32[]{:S(2)}) async-start(), calls=%async_computation.5 | async-start | bytes 147456
  6.5 24.4 %collective-permute-start = (bf16[64,8,128]{2,1,0:T(8,128)(2,1)}, bf16[64,8,128]{2,1,0:T(8,128)(2,1)S(1)}, u32[]{:S(2)}, u32[]{:S(2)}) collective-permute-start(bf16[64,8,128]{2,1,0:T(8,128)(2,1)} %param.10), channel_id=1, source_target_pairs={{0,4},{4,8},{8,12},{12,16},{16,20},{20,24},{24,28},{28,0},{1,5},{5... | collective-permute-start | bytes 393224 | tf_op jit(solution)/shard_map/ppermute | solution.py:73
  7.0 24.0 %collective-permute-start.1 = (bf16[64,8,128]{2,1,0:T(8,128)(2,1)}, bf16[64,8,128]{2,1,0:T(8,128)(2,1)S(1)}, u32[]{:S(2)}, u32[]{:S(2)}) collective-permute-start(bf16[64,8,128]{2,1,0:T(8,128)(2,1)} %param.10), channel_id=1, source_target_pairs={{0,28},{4,0},{8,4},{12,8},{16,12},{20,16},{24,20},{28,24},{1,29},{... | collective-permute-start | bytes 393224 | tf_op jit(solution)/shard_map/ppermute | solution.py:78
  21.5 9.4 %copy-start.1 = (bf16[64,8,128]{2,1,0:T(8,128)(2,1)S(1)}, bf16[64,8,128]{2,1,0:T(8,128)(2,1)}, u32[]{:S(2)}) copy-start(bf16[64,8,128]{2,1,0:T(8,128)(2,1)} %param.10) | copy-start | bytes 393220
  21.5 9.4 %copy-start.3 = (s32[512]{0:T(512)S(1)}, s32[512]{0:T(512)}, u32[]{:S(2)}) copy-start(s32[512]{0:T(512)} %param.14) | copy-start | bytes 6148
  31.0 5.3 %collective-permute-start.2 = (bf16[64,8,128]{2,1,0:T(8,128)(2,1)S(1)}, bf16[64,8,128]{2,1,0:T(8,128)(2,1)S(1)}, u32[]{:S(2)}, u32[]{:S(2)}) collective-permute-start(bf16[64,8,128]{2,1,0:T(8,128)(2,1)S(1)} %collective-permute-done), channel_id=1, source_target_pairs={{0,4},{4,8},{8,12},{12,16},{16,20},{20,24},{24,28},{28,0},{1,5},{5... | collective-permute-start | bytes 393224 | tf_op jit(solution)/shard_map/ppermute | solution.py:73
  31.0 5.3 %collective-permute-start.3 = (bf16[64,8,128]{2,1,0:T(8,128)(2,1)S(1)}, bf16[64,8,128]{2,1,0:T(8,128)(2,1)S(1)}, u32[]{:S(2)}, u32[]{:S(2)}) collective-permute-start(bf16[64,8,128]{2,1,0:T(8,128)(2,1)S(1)} %collective-permute-done.1), channel_id=1, source_target_pairs={{0,28},{4,0},{8,4},{12,8},{16,12},{20,16},{24,20},{28,24},{1,29},{... | collective-permute-start | bytes 393224 | tf_op jit(solution)/shard_map/ppermute | solution.py:78
  36.3 5.6 %collective-permute-start.4 = (bf16[64,8,128]{2,1,0:T(8,128)(2,1)S(1)}, bf16[64,8,128]{2,1,0:T(8,128)(2,1)S(1)}, u32[]{:S(2)}, u32[]{:S(2)}) collective-permute-start(bf16[64,8,128]{2,1,0:T(8,128)(2,1)S(1)} %collective-permute-done.2), channel_id=1, source_target_pairs={{0,4},{4,8},{8,12},{12,16},{16,20},{20,24},{24,28},{28,0},{1,5},{5... | collective-permute-start | bytes 393224 | tf_op jit(solution)/shard_map/ppermute | solution.py:73
  36.3 5.6 %collective-permute-start.5 = (bf16[64,8,128]{2,1,0:T(8,128)(2,1)S(1)}, bf16[64,8,128]{2,1,0:T(8,128)(2,1)S(1)}, u32[]{:S(2)}, u32[]{:S(2)}) collective-permute-start(bf16[64,8,128]{2,1,0:T(8,128)(2,1)S(1)} %collective-permute-done.3), channel_id=1, source_target_pairs={{0,28},{4,0},{8,4},{12,8},{16,12},{20,16},{24,20},{28,24},{1,29},{... | collective-permute-start | bytes 393224 | tf_op jit(solution)/shard_map/ppermute | solution.py:78
  41.9 5.3 %collective-permute-start.6 = (bf16[64,8,128]{2,1,0:T(8,128)(2,1)S(1)}, bf16[64,8,128]{2,1,0:T(8,128)(2,1)S(1)}, u32[]{:S(2)}, u32[]{:S(2)}) collective-permute-start(bf16[64,8,128]{2,1,0:T(8,128)(2,1)S(1)} %collective-permute-done.4), channel_id=1, source_target_pairs={{0,4},{4,8},{8,12},{12,16},{16,20},{20,24},{24,28},{28,0},{1,5},{5... | collective-permute-start | bytes 393224 | tf_op jit(solution)/shard_map/ppermute | solution.py:73
  57.6 75.5 %reduce-scatter.6.cloned.1.call-start = ((), (), s32[]{:S(2)}) async-start(), calls=%async_computation.3 | async-start | bytes 1179648 | tf_op jit(solution)/shard_map/reduce_scatter | solution.py:89
  57.6 10.3 %copy-start.4 = (s32[64]{0:T(128)S(1)}, s32[64]{0:T(128)}, u32[]{:S(2)}) copy-start(s32[64]{0:T(128)} %param.16) | copy-start | bytes 772
  67.7 95.1 %reduce-scatter.8.cloned.1.call-start = ((), (), s32[]{:S(2)}) async-start(), calls=%async_computation.4 | async-start | bytes 737280 | tf_op jit(solution)/shard_map/reduce_scatter | solution.py:103
  81.8 82.1 %copy-start = (bf16[16,4608]{1,0:T(8,128)(2,1)S(1)}, bf16[16,4608]{1,0:T(8,128)(2,1)}, u32[]{:S(2)}) copy-start(bf16[16,4608]{1,0:T(8,128)(2,1)} %param.18) | copy-start | bytes 442372
  81.8 82.1 %copy-start.2 = (f32[4608]{0:T(1024)S(1)}, f32[4608]{0:T(1024)}, u32[]{:S(2)}) copy-start(f32[4608]{0:T(1024)} %param.19) | copy-start | bytes 55300
Sparse Core Ops, SparseCore 0:
  57.7 36.1 reduce-scatter.9
  97.0 35.9 reduce-scatter.5
  140.7 22.1 reduce-scatter.7
